TPU v7x, 8 devices: a whole 2x2x1 slice. The times are simulated.
8 devices in a mesh: dp: 1 (over z), tp: 8 (over y, x, core).
Axes of the slice: x: 2, y: 2, z: 1, core: 2. Of those that a mesh axis runs over, the one named last changes fastest.
Arguments:
- resid_in: bfloat16 [128, 8192], P('dp')
- positions: int32 [128], P('dp')
- k_cache: bfloat16 [128, 128, 8, 128], P('dp', None, 'tp')
- v_cache: bfloat16 [128, 128, 8, 128], P('dp', None, 'tp')
- gain_attn: bfloat16 [8192], replicated
- w_query: bfloat16 [8192, 8192], P(None, 'tp')
- w_key: bfloat16 [8192, 1024], P(None, 'tp')
- w_value: bfloat16 [8192, 1024], P(None, 'tp')
- w_out: bfloat16 [8192, 8192], P('tp')
- gain_mlp: bfloat16 [8192], replicated
- w_gate: bfloat16 [8192, 22016], P(None, 'tp')
- w_up: bfloat16 [8192, 22016], P(None, 'tp')
- w_down: bfloat16 [22016, 8192], P('tp')
Outputs:
- output 1: bfloat16 [128, 8192], P('dp')
- output 2: bfloat16 [128, 128, 8, 128], P('dp', None, 'tp')
- output 3: bfloat16 [128, 128, 8, 128], P('dp', None, 'tp')
All inputs are finite; a program needn't handle non-finite values.
Results may differ from a plain program's by a relative error of at most 0.010786.
Values sent between devices are 32-bit elements.
A program may use at most 1 GiB of HBM per device.

v0:
```python
import math
import jax
import jax.numpy as jnp
from jax import lax
from jax.sharding import PartitionSpec as P

EPS = 1e-5
ROPE_THETA = 500000.0
ROPE_FACTOR = 8.0
LOW_FACTOR = 1.0
HIGH_FACTOR = 4.0
ORIG_CTX = 8192.0


def rms_norm(rows_in, gain):
    rows_f = rows_in.astype(jnp.float32)
    mean_sq = jnp.mean(rows_f * rows_f, axis=-1, keepdims=True)
    return (rows_f * lax.rsqrt(mean_sq + EPS) * gain.astype(jnp.float32)).astype(jnp.bfloat16)


def rope_tables(positions, head_dim):
    half_dim = head_dim // 2
    exponents = jnp.arange(half_dim, dtype=jnp.float32) * (2.0 / head_dim)
    inv_freq = 1.0 / jnp.power(ROPE_THETA, exponents)
    wavelen = (2.0 * math.pi) / inv_freq
    smooth = (ORIG_CTX / wavelen - LOW_FACTOR) / (HIGH_FACTOR - LOW_FACTOR)
    blended = (1.0 - smooth) * inv_freq / ROPE_FACTOR + smooth * inv_freq
    inv_freq = jnp.where(wavelen < ORIG_CTX / HIGH_FACTOR, inv_freq,
                         jnp.where(wavelen > ORIG_CTX / LOW_FACTOR, inv_freq / ROPE_FACTOR, blended))
    angles = positions.astype(jnp.float32)[:, None] * inv_freq[None, :]
    return jnp.cos(angles), jnp.sin(angles)


def apply_rope(vectors, cos_t, sin_t):
    half_dim = vectors.shape[-1] // 2
    lower_half = vectors[..., :half_dim]
    upper_half = vectors[..., half_dim:]
    cos_b = cos_t[:, None, :]
    sin_b = sin_t[:, None, :]
    return jnp.concatenate([lower_half * cos_b - upper_half * sin_b,
                            upper_half * cos_b + lower_half * sin_b], axis=-1)


def attention_block(resid_in, positions, k_cache, v_cache, gain_attn, w_query, w_key, w_value):
    n_seqs = resid_in.shape[0]
    cache_len = k_cache.shape[1]
    kv_heads = k_cache.shape[2]
    head_dim = k_cache.shape[3]
    group_size = w_query.shape[1] // (kv_heads * head_dim)
    normed = rms_norm(resid_in, gain_attn)
    queries = jnp.dot(normed, w_query, preferred_element_type=jnp.float32).astype(jnp.bfloat16)
    key_new = jnp.dot(normed, w_key, preferred_element_type=jnp.float32).astype(jnp.bfloat16)
    value_new = jnp.dot(normed, w_value, preferred_element_type=jnp.float32).astype(jnp.bfloat16)
    cos_t, sin_t = rope_tables(positions, head_dim)
    queries = apply_rope(queries.reshape(n_seqs, kv_heads * group_size, head_dim).astype(jnp.float32), cos_t, sin_t)
    queries = queries.astype(jnp.bfloat16).reshape(n_seqs, kv_heads, group_size, head_dim)
    key_new = apply_rope(key_new.reshape(n_seqs, kv_heads, head_dim).astype(jnp.float32), cos_t, sin_t)
    key_new = key_new.astype(jnp.bfloat16)
    value_new = value_new.reshape(n_seqs, kv_heads, head_dim)
    slot_iota = lax.broadcasted_iota(jnp.int32, (n_seqs, cache_len), 1)
    slot_hit = (slot_iota == positions[:, None])[:, :, None, None]
    k_full = jnp.where(slot_hit, key_new[:, None], k_cache)
    v_full = jnp.where(slot_hit, value_new[:, None], v_cache)
    scores = jnp.einsum('bkgd,bskd->bkgs', queries, k_full, preferred_element_type=jnp.float32)
    scores = scores * (1.0 / math.sqrt(head_dim))
    valid = (slot_iota <= positions[:, None])[:, None, None, :]
    scores = jnp.where(valid, scores, -jnp.inf)
    attn_prob = jax.nn.softmax(scores, axis=-1).astype(jnp.bfloat16)
    attn_out = jnp.einsum('bkgs,bskd->bkgd', attn_prob, v_full, preferred_element_type=jnp.float32)
    attn_out = attn_out.astype(jnp.bfloat16).reshape(n_seqs, kv_heads * group_size * head_dim)
    return attn_out, k_full, v_full


def gated_hidden(normed, w_gate, w_up):
    gate_proj = jnp.dot(normed, w_gate, preferred_element_type=jnp.float32).astype(jnp.bfloat16)
    up_proj = jnp.dot(normed, w_up, preferred_element_type=jnp.float32).astype(jnp.bfloat16)
    return (jax.nn.silu(gate_proj.astype(jnp.float32)) * up_proj.astype(jnp.float32)).astype(jnp.bfloat16)


def solution(mesh):
    def layer_local(resid_in, positions, k_cache, v_cache, gain_attn, w_query, w_key, w_value,
                    w_out, gain_mlp, w_gate, w_up, w_down):
        attn_out, k_full, v_full = attention_block(resid_in, positions, k_cache, v_cache,
                                                   gain_attn, w_query, w_key, w_value)
        y_part = jnp.dot(attn_out, w_out, preferred_element_type=jnp.float32)
        y_sum = lax.psum(y_part, 'tp')
        resid_mid = (resid_in.astype(jnp.float32) + y_sum).astype(jnp.bfloat16)
        hidden = gated_hidden(rms_norm(resid_mid, gain_mlp), w_gate, w_up)
        z_part = jnp.dot(hidden, w_down, preferred_element_type=jnp.float32)
        z_sum = lax.psum(z_part, 'tp')
        resid_out = (resid_mid.astype(jnp.float32) + z_sum).astype(jnp.bfloat16)
        return resid_out, k_full, v_full

    row_spec = P('dp', None)
    cache_spec = P('dp', None, 'tp', None)
    col_spec = P(None, 'tp')
    split_rows = P('tp', None)
    return jax.shard_map(layer_local, mesh=mesh,
                         in_specs=(row_spec, P('dp'), cache_spec, cache_spec, P(), col_spec, col_spec,
                                   col_spec, split_rows, P(), col_spec, col_spec, split_rows),
                         out_specs=(row_spec, cache_spec, cache_spec), check_vma=False)
```

profile of v0, /device:TPU:0, one launch (start us, length us, event | category | flops | bytes accessed | tf_op | source)
XLA Modules:
  0.0 267.0 jit_solution(17850527452463531089)
XLA Ops:
  7.3 0.8 convert_element_type.89
  8.1 1.2 iota_compare_fusion.1
  9.3 2.1 fusion.1
  11.4 0.7 convert_element_type.84
  12.1 2.4 convolution_convert_fusion.3
  14.5 1.1 fusion.37
  15.7 0.3 multiply_cosine_fusion
  16.0 0.2 fusion.58
  16.4 8.3 %fusion.35 = f32[16,8,8,128]{3,1,2,0:T(8,128)S(1)} fusion(bf16[8192,1024]{1,0:T(8,128)(2,1)} %param.18, bf16[128,8192]{1,0:T(8,128)(2,1)S(1)} %copy-done.5, f32[8192]{0:T(1024)S(1)} %convert_element_type.84, f32[128]{0:T(128)S(1)} %add_rsqrt_fusion.1), kind=kOutput, calls=%fused_computation.40 | convolution fusion | flops 2151940096 | bytes 19431936 | tf_op jit(solution)/shard_map/dot_general | solution.py:51
  24.8 0.3 subtract_convert_fusion
  25.1 4.9 %broadcast_select_fusion.1 = (bf16[128,128,1,128]{3,1,2,0:T(8,128)(2,1)S(1)}, bf16[128,128,1,128]{3,1,2,0:T(8,128)(2,1)}) fusion(bf16[128,128,1,128]{3,1,2,0:T(8,128)(2,1)S(1)} %copy-done.6, pred[128,128]{1,0:T(8,128)(4,1)S(1)} %get-tuple-element.14, bf16[128,128]{1,0:T(8,128)(2,1)S(1)} %copy.16, bf16[128,128,1,128]{3,1,2,0:T(8,128)(2,1)S(1)} %copy-done.7, ...), kind=kLoop, calls=%fused_computation.20 | loop fusion | flops 4194304 | bytes 16859136 | tf_op jit(solution)/shard_map/jit(_where)/select_n | solution.py:62
  30.0 2.0 copy-done.3
  32.0 2.3 fusion.28
  34.3 0.4 fusion.65
  34.7 4.0 %fusion.31 = bf16[128,8,128]{2,1,0:T(8,128)(2,1)S(1)} fusion(bf16[128,128,1,128]{3,1,2,0:T(8,128)(2,1)} %get-tuple-element.10, f32[128,8]{1,0:T(8,128)S(1)} %fusion.65, f32[128,8,128]{2,1,0:T(8,128)S(1)} %fusion.28), kind=kOutput, calls=%fused_computation.37 | convolution fusion | flops 34079872 | bytes 4984832 | tf_op jit(solution)/shard_map/bkgs,bskd->bkgd/dot_general | solution.py:69
  38.7 10.1 %fusion.42 = f32[128,8192]{1,0:T(8,128)} fusion(bf16[1024,8192]{1,0:T(8,128)(2,1)} %param.21, bf16[16,8,8,128]{3,2,1,0:T(8,128)(2,1)S(1)} %bitcast.38), kind=kOutput, calls=%fused_computation.49 | convolution fusion | flops 2147483648 | bytes 21233664 | tf_op jit(solution)/shard_map/dot_general | solution.py:85
  48.8 0.2 all-reduce.5.cloned.1.call-start
  49.0 0.5 copy-done.8
  49.5 71.6 %all-reduce.3.cloned.1.call-done = f32[128,8192]{1,0:T(8,128)} async-done(((f32[128,8192]{1,0:T(8,128)}), f32[128,8192]{1,0:T(8,128)}) %all-reduce.3.cloned.1.call-update) | async-done | bytes 4194320 | tf_op jit(solution)/shard_map/psum | solution.py:86
  121.0 3.6 %fusion.5 = (f32[128]{0:T(128)S(1)}, bf16[128,8192]{1,0:T(8,128)(2,1)S(1)}) fusion(f32[128,8192]{1,0:T(8,128)} %all-reduce.3.cloned.1.call-done, bf16[128,8192]{1,0:T(8,128)(2,1)} %param.13), kind=kLoop, calls=%fused_computation.11 | loop fusion | flops 6291328 | bytes 8389120 | tf_op jit(solution)/shard_map/reduce_sum | solution.py:17
  124.6 19.6 %fusion.13 = f32[128,2752]{0,1:T(8,128)S(1)} fusion(bf16[8192,2752]{0,1:T(8,128)(2,1)} %param.23, bf16[128,8192]{1,0:T(8,128)(2,1)S(1)} %get-tuple-element.4, f32[8192]{0:T(1024)S(1)} %convert_element_type.98, f32[128]{0:T(128)S(1)} %add_rsqrt_fusion), kind=kOutput, calls=%fused_computation.23 | convolution fusion | flops 5776261120 | bytes 48628224 | tf_op jit(solution)/shard_map/dot_general | solution.py:75
  144.2 41.8 %fusion.17 = f32[128,8192]{1,0:T(8,128)} fusion(bf16[2752,8192]{1,0:T(8,128)(2,1)} %param.25, bf16[8192,2752]{0,1:T(8,128)(2,1)} %param.24, f32[128,2752]{0,1:T(8,128)S(1)} %fusion.13, bf16[128,8192]{1,0:T(8,128)(2,1)S(1)} %get-tuple-element.4, f32[8192]{0:T(1024)S(1)} %convert_element_type.98, f32[128]{0:T(128)S(1)} %add_rsqrt_fusion), kind=kOutput, calls=%fused_computation.27 | convolution fusion | flops 11549736960 | bytes 97911296 | tf_op jit(solution)/shard_map/dot_general | solution.py:89
  186.1 69.5 %all-reduce.5.cloned.1.call-done = f32[128,8192]{1,0:T(8,128)} async-done(((f32[128,8192]{1,0:T(8,128)}), f32[128,8192]{1,0:T(8,128)}) %all-reduce.5.cloned.1.call-update) | async-done | bytes 4194320 | tf_op jit(solution)/shard_map/psum | solution.py:90
  255.6 4.6 %fusion.8 = bf16[128,8192]{1,0:T(8,128)(2,1)} fusion(f32[128,8192]{1,0:T(8,128)} %all-reduce.5.cloned.1.call-done, bf16[128,8192]{1,0:T(8,128)(2,1)} %copy-done.2), kind=kLoop, calls=%fused_computation.14 | loop fusion | flops 3145728 | bytes 8388608 | tf_op jit(solution)/shard_map/convert_element_type | solution.py:91
  (28 shorter events, 0.4 us)
Async XLA Ops:
  7.2 4.9 %copy-start = (bf16[8192,128]{1,0:T(8,128)(2,1)S(1)}, bf16[8192,128]{1,0:T(8,128)(2,1)}, u32[]{:S(2)}) copy-start(bf16[8192,128]{1,0:T(8,128)(2,1)} %param.20) | copy-start | bytes 6291460
  7.2 113.8 %all-reduce.3.cloned.1.call-start = ((), (), s32[]{:S(2)}) async-start(), calls=%async_computation | async-start | bytes 8388608 | tf_op jit(solution)/shard_map/psum | solution.py:86
  7.2 7.3 %copy-start.4 = (bf16[128,8192]{1,0:T(8,128)(2,1)S(1)}, bf16[128,8192]{1,0:T(8,128)(2,1)}, u32[]{:S(2)}) copy-start(bf16[128,8192]{1,0:T(8,128)(2,1)} %param.13) | copy-start | bytes 6291460
  7.2 7.3 %copy-start.9 = (bf16[8192,128]{1,0:T(8,128)(2,1)S(1)}, bf16[8192,128]{1,0:T(8,128)(2,1)}, u32[]{:S(2)}) copy-start(bf16[8192,128]{1,0:T(8,128)(2,1)} %param.19) | copy-start | bytes 6291460
  14.5 1.8 copy-start.5
  16.3 8.7 %copy-start.6 = (bf16[128,128,1,128]{3,1,2,0:T(8,128)(2,1)S(1)}, bf16[128,128,1,128]{3,1,2,0:T(8,128)(2,1)}, u32[]{:S(2)}) copy-start(bf16[128,128,1,128]{3,1,2,0:T(8,128)(2,1)} %param.15) | copy-start | bytes 12582916
  16.4 8.7 %copy-start.7 = (bf16[128,128,1,128]{3,1,2,0:T(8,128)(2,1)S(1)}, bf16[128,128,1,128]{3,1,2,0:T(8,128)(2,1)}, u32[]{:S(2)}) copy-start(bf16[128,128,1,128]{3,1,2,0:T(8,128)(2,1)} %param.16) | copy-start | bytes 12582916
  30.0 2.0 copy-start.3
  48.8 0.7 copy-start.8
  48.8 206.8 %all-reduce.5.cloned.1.call-start = ((), (), s32[]{:S(2)}) async-start(), calls=%async_computation.1 | async-start | bytes 8388608 | tf_op jit(solution)/shard_map/psum | solution.py:90
  124.6 19.6 %copy-start.2 = (bf16[128,8192]{1,0:T(8,128)(2,1)}, bf16[128,8192]{1,0:T(8,128)(2,1)S(1)}, u32[]{:S(2)}) copy-start(bf16[128,8192]{1,0:T(8,128)(2,1)S(1)} %get-tuple-element.4) | copy-start | bytes 6291460
  186.1 74.1 %copy-start.1 = (bf16[8192,128]{1,0:T(8,128)(2,1)S(1)}, bf16[8192,128]{1,0:T(8,128)(2,1)}, u32[]{:S(2)}) copy-start(bf16[8192,128]{1,0:T(8,128)(2,1)} %param.20) | copy-start | bytes 6291460
Sparse Core Ops, SparseCore 0:
  48.9 72.0 all-reduce.2
  186.2 69.3 all-reduce.4
where the time goes:
time: 267 us
  waiting for transfers between devices  141 us (53%)
  matrix products  89.6 us (34%)
  other arithmetic  19.1 us (7%)
  between operations  14.3 us (5%)
  local copies, waits for them, and re-layouts  2.73 us (1%)
    psum x1, waiting for transfers between devices, layer_local(): y_sum = lax.psum(y_part, 'tp')  71.6 us
    psum x1, waiting for transfers between devices, layer_local(): z_sum = lax.psum(z_part, 'tp')  69.5 us
    dot_general x1, matrix products, layer_local(): z_part = jnp.dot(hidden, w_down, preferred_element_type=jnp.float32)  41.8 us
    dot_general x1, matrix products, gated_hidden(): jnp.dot(normed, w_gate, preferred_element_type=jnp.float32)  19.6 us
    dot_general x1, matrix products, layer_local(): y_part = jnp.dot(attn_out, w_out, preferred_element_type=jnp.float32)  10.1 us
    dot_general x1, matrix products, attention_block(): jnp.dot(normed, w_query, preferred_element_type=jnp.float32)  8.3 us
    reduce_sum x2, other arithmetic, rms_norm(): mean_sq = jnp.mean(rows_f * rows_f, axis=-1, keepdims=True)  5.66 us
  transfers between devices with their start and end apart: 2, of which 2 were waited for; matrix products, arithmetic and copies ran while one was open for 0% of the time, Pallas kernels for 0%

commit v1 on v0

--- a/solution.py
+++ b/solution.py
@@ -2,6 +2,8 @@
 import jax
 import jax.numpy as jnp
 from jax import lax
+from jax.experimental import pallas as pl
+from jax.experimental.pallas import tpu as pltpu
 from jax.sharding import PartitionSpec as P
 
 EPS = 1e-5
@@ -71,10 +73,316 @@
     return attn_out, k_full, v_full
 
 
-def gated_hidden(normed, w_gate, w_up):
-    gate_proj = jnp.dot(normed, w_gate, preferred_element_type=jnp.float32).astype(jnp.bfloat16)
-    up_proj = jnp.dot(normed, w_up, preferred_element_type=jnp.float32).astype(jnp.bfloat16)
-    return (jax.nn.silu(gate_proj.astype(jnp.float32)) * up_proj.astype(jnp.float32)).astype(jnp.bfloat16)
+N_CHUNK = 16
+N_SLOT = 15
+MESH = pl.DeviceIdType.MESH
+
+
+def tail_kernel(attn_ref, resid_hbm, gain_ref, w_out_hbm, gate_t_hbm, up_t_hbm, w_down_hbm, out_ref,
+                part, from_core, from_x1, from_y1, from_x2, from_y2, gathered, mid, sq_sum, resid_own,
+                gate_acc, up_acc, hidden, ring,
+                resid_sem, out_sem, ring_sem, rs_send, rs_recv, ag_send, ag_recv):
+    n_chunk, chunk = N_CHUNK, part.shape[-1]
+    half = chunk // 2
+    rows = mid.shape[1]
+    me = lax.axis_index('tp')
+    k = me % 2
+    x = (me // 2) % 2
+    y = me // 4
+    nk, nx, ny = 1 - k, 1 - x, 1 - y
+    core_nbr = {'tp': me + 1 - 2 * k}
+    x_nbr = {'tp': me + 2 - 4 * x}
+    y_nbr = {'tp': me + 4 - 8 * y}
+
+    def cols(c):
+        return pl.ds(pl.multiple_of(c * chunk, chunk), chunk)
+
+    depth_out = w_out_hbm.shape[0]
+    first_mlp = n_chunk // 2
+    first_down = first_mlp + 2 * n_chunk
+
+    def out_slot(c):
+        return c // 2, pl.ds(pl.multiple_of((c % 2) * depth_out, depth_out), depth_out)
+
+    def out_copy(c):
+        slot, span = out_slot(c)
+        return pltpu.make_async_copy(w_out_hbm.at[:, cols(c)], ring.at[slot, span], out_sem.at[c])
+
+    def ring_copy(src, c, j):
+        slot = j % N_SLOT
+        return pltpu.make_async_copy(src.at[:, cols(c)], ring.at[slot], ring_sem.at[slot])
+
+    def gate_copy(c):
+        return ring_copy(gate_t_hbm, c, first_mlp + 2 * c)
+
+    def up_copy(c):
+        return ring_copy(up_t_hbm, c, first_mlp + 2 * c + 1)
+
+    def down_copy(c):
+        return ring_copy(w_down_hbm, c, first_down + c)
+
+    def start_load(j):
+        m = j - first_mlp
+
+        @pl.when(j < first_down)
+        def _():
+            @pl.when(m % 2 == 0)
+            def _():
+                gate_copy(m // 2).start()
+
+            @pl.when(m % 2 == 1)
+            def _():
+                up_copy(m // 2).start()
+
+        @pl.when(jnp.logical_and(j >= first_down, j < first_down + n_chunk))
+        def _():
+            down_copy(j - first_down).start()
+
+    row0 = pl.multiple_of(64 * k + 32 * x + 16 * y, 16)
+    resid_copy = pltpu.make_async_copy(resid_hbm.at[pl.ds(row0, rows)], resid_own, resid_sem)
+    for c in range(2):
+        out_copy(c).start()
+    resid_copy.start()
+    for c in range(2, n_chunk):
+        out_copy(c).start()
+    for j in range(first_mlp, N_SLOT):
+        (up_copy if (j - first_mlp) % 2 else gate_copy)((j - first_mlp) // 2).start()
+
+    barrier = pltpu.get_barrier_semaphore()
+    for nbr in (core_nbr, x_nbr, y_nbr):
+        pl.semaphore_signal(barrier, inc=1, device_id=nbr, device_id_type=MESH)
+
+    def remote(src, dst, sems, ch, c, nbr):
+        return pltpu.make_async_remote_copy(src_ref=src, dst_ref=dst, send_sem=sems[0].at[ch, c],
+                                            recv_sem=sems[1].at[ch, c], device_id=nbr, device_id_type=MESH)
+
+    rs = (rs_send, rs_recv)
+    ag = (ag_send, ag_recv)
+    left, right = pl.ds(0, half), pl.ds(half, half)
+
+    def rs_core(c):
+        return remote(part.at[c, nk], from_core.at[c], rs, 0, c, core_nbr)
+
+    def rs_x1(c):
+        return remote(part.at[c, k, nx, :, :, left], from_x1.at[c], rs, 1, c, x_nbr)
+
+    def rs_y1(c):
+        return remote(part.at[c, k, :, ny, :, right], from_y1.at[c], rs, 2, c, y_nbr)
+
+    def rs_y2(c):
+        return remote(part.at[c, k, x, ny, :, left], from_y2.at[c], rs, 3, c, y_nbr)
+
+    def rs_x2(c):
+        return remote(part.at[c, k, nx, y, :, right], from_x2.at[c], rs, 4, c, x_nbr)
+
+    def ag_x(c):
+        blk = gathered.at[c, k, x, y]
+        return remote(blk, blk, ag, 0, c, x_nbr)
+
+    def ag_y(c):
+        blk = gathered.at[c, k, x, y]
+        return remote(blk, blk, ag, 1, c, y_nbr)
+
+    def ag_fwd_y(c):
+        blk = gathered.at[c, k, nx, y, :, right]
+        return remote(blk, blk, ag, 2, c, y_nbr)
+
+    def ag_fwd_x(c):
+        blk = gathered.at[c, k, x, ny, :, left]
+        return remote(blk, blk, ag, 3, c, x_nbr)
+
+    def ag_core(c):
+        blk = gathered.at[c, k]
+        return remote(blk, blk, ag, 4, c, core_nbr)
+
+    def stage(s, lag, fn):
+        c = s - lag
+
+        @pl.when(jnp.logical_and(c >= 0, c < n_chunk))
+        def _():
+            fn(c)
+
+    def rs_stage1(c):
+        rs_core(c).wait_recv()
+        part[c, k] = part[c, k] + from_core[c]
+        rs_x1(c).start()
+        rs_y1(c).start()
+
+    def rs_stage2(c):
+        rs_x1(c).wait_recv()
+        part[c, k, x, :, :, left] = part[c, k, x, :, :, left] + from_x1[c]
+        rs_y2(c).start()
+        rs_y1(c).wait_recv()
+        part[c, k, :, y, :, right] = part[c, k, :, y, :, right] + from_y1[c]
+        rs_x2(c).start()
+
+    def rs_stage3(c):
+        rs_y2(c).wait_recv()
+        rs_x2(c).wait_recv()
+        total = jnp.concatenate([part[c, k, x, y, :, left] + from_y2[c],
+                                 part[c, k, x, y, :, right] + from_x2[c]], axis=-1)
+        for copy in (rs_core, rs_x1, rs_y1, rs_y2, rs_x2):
+            copy(c).wait_send()
+        return total
+
+    def ag_stage1(c):
+        ag_x(c).wait_recv()
+        ag_fwd_y(c).start()
+        ag_y(c).wait_recv()
+        ag_fwd_x(c).start()
+
+    def ag_stage2(c):
+        ag_fwd_x(c).wait_recv()
+        ag_fwd_y(c).wait_recv()
+        ag_core(c).start()
+
+    def ag_stage3(c):
+        ag_core(c).wait_recv()
+        block = gathered[c].reshape(8 * rows, chunk)
+        for copy in (ag_x, ag_y, ag_fwd_x, ag_fwd_y, ag_core):
+            copy(c).wait_send()
+        return block
+
+    pl.semaphore_wait(barrier, 3)
+    sq_sum[...] = jnp.zeros_like(sq_sum)
+    resid_copy.wait()
+
+    def proj(c):
+        out_copy(c).wait()
+        slot, span = out_slot(c)
+        res = jnp.dot(attn_ref[...], ring[slot, span], preferred_element_type=jnp.float32)
+        part[c] = res.reshape(part.shape[1:])
+        rs_core(c).start()
+
+        @pl.when(c % 2 == 1)
+        def _():
+            start_load(c // 2 + N_SLOT)
+
+    def finish_mid(c):
+        total = rs_stage3(c)
+        x1 = (resid_own[:, cols(c)].astype(jnp.float32) + total).astype(jnp.bfloat16).astype(jnp.float32)
+        mid[c] = x1
+        sq_sum[...] += x1 * x1
+
+    def rs_body(s, carry):
+        stage(s, RS_LAG[0], rs_stage1)
+        stage(s, RS_LAG[1], rs_stage2)
+        stage(s, RS_LAG[2], finish_mid)
+        stage(s, 0, proj)
+        return carry
+
+    lax.fori_loop(0, n_chunk + RS_LAG[2], rs_body, 0)
+
+    mean_sq = jnp.sum(sq_sum[...], axis=-1, keepdims=True) * (1.0 / (n_chunk * chunk))
+    scale = lax.rsqrt(mean_sq + EPS)
+    gate_acc[...] = jnp.zeros_like(gate_acc)
+    up_acc[...] = jnp.zeros_like(up_acc)
+
+    def send_normed(c):
+        normed = (mid[c] * scale * gain_ref[:, cols(c)].astype(jnp.float32)).astype(jnp.bfloat16)
+        gathered[c, k, x, y] = normed.astype(jnp.float32)
+        ag_x(c).start()
+        ag_y(c).start()
+
+    def gate_up(c):
+        block = ag_stage3(c).astype(jnp.bfloat16)
+        for copy, acc, j in ((gate_copy, gate_acc, first_mlp + 2 * c), (up_copy, up_acc, first_mlp + 2 * c + 1)):
+            copy(c).wait()
+            acc[...] += lax.dot_general(block, ring[j % N_SLOT], (((1,), (1,)), ((), ())),
+                                        preferred_element_type=jnp.float32)
+            start_load(j + N_SLOT)
+
+    def ag_body(s, carry):
+        stage(s, AG_LAG[0], ag_stage1)
+        stage(s, AG_LAG[1], ag_stage2)
+        stage(s, 0, send_normed)
+        stage(s, AG_LAG[2], gate_up)
+        return carry
+
+    lax.fori_loop(0, n_chunk + AG_LAG[2], ag_body, 0)
+
+    gate = gate_acc[...].astype(jnp.bfloat16).astype(jnp.float32)
+    up = up_acc[...].astype(jnp.bfloat16).astype(jnp.float32)
+    hidden[...] = (jax.nn.silu(gate) * up).astype(jnp.bfloat16)
+
+    def down(c):
+        down_copy(c).wait()
+        j = first_down + c
+        res = jnp.dot(hidden[...], ring[j % N_SLOT], preferred_element_type=jnp.float32)
+        part[c] = res.reshape(part.shape[1:])
+        rs_core(c).start()
+        start_load(j + N_SLOT)
+
+    def finish_out(c):
+        total = rs_stage3(c)
+        gathered[c, k, x, y] = (mid[c] + total).astype(jnp.bfloat16).astype(jnp.float32)
+        ag_x(c).start()
+        ag_y(c).start()
+
+    def store_out(c):
+        out_ref[:, cols(c)] = ag_stage3(c).astype(jnp.bfloat16)
+
+    base = RS_LAG[2]
+
+    def down_body(s, carry):
+        stage(s, RS_LAG[0], rs_stage1)
+        stage(s, RS_LAG[1], rs_stage2)
+        stage(s, base, finish_out)
+        stage(s, base + AG_LAG[0], ag_stage1)
+        stage(s, base + AG_LAG[1], ag_stage2)
+        stage(s, 0, down)
+        stage(s, base + AG_LAG[2], store_out)
+        return carry
+
+    lax.fori_loop(0, n_chunk + base + AG_LAG[2], down_body, 0)
+
+
+RS_LAG = (1, 4, 7)
+AG_LAG = (3, 6, 8)
+
+
+def layer_tail(attn_out, resid_in, gain_mlp, w_out, w_gate, w_up, w_down):
+    n_rows, width = resid_in.shape
+    ffn = w_gate.shape[1]
+    chunk = width // N_CHUNK
+    half = chunk // 2
+    rows = n_rows // 8
+    f32, bf16 = jnp.float32, jnp.bfloat16
+    vmem = pl.BlockSpec(memory_space=pltpu.VMEM)
+    hbm = pl.BlockSpec(memory_space=pl.ANY)
+    dma = pltpu.SemaphoreType.DMA
+    return pl.pallas_call(
+        tail_kernel,
+        out_shape=jax.ShapeDtypeStruct((n_rows, width), bf16),
+        in_specs=[vmem, hbm, vmem, hbm, hbm, hbm, hbm],
+        out_specs=vmem,
+        scratch_shapes=[
+            pltpu.VMEM((N_CHUNK, 2, 2, 2, rows, chunk), f32),
+            pltpu.VMEM((N_CHUNK, 2, 2, rows, chunk), f32),
+            pltpu.VMEM((N_CHUNK, 2, rows, half), f32),
+            pltpu.VMEM((N_CHUNK, 2, rows, half), f32),
+            pltpu.VMEM((N_CHUNK, rows, half), f32),
+            pltpu.VMEM((N_CHUNK, rows, half), f32),
+            pltpu.VMEM((N_CHUNK, 2, 2, 2, rows, chunk), f32),
+            pltpu.VMEM((N_CHUNK, rows, chunk), f32),
+            pltpu.VMEM((rows, chunk), f32),
+            pltpu.VMEM((rows, width), bf16),
+            pltpu.VMEM((n_rows, ffn), f32),
+            pltpu.VMEM((n_rows, ffn), f32),
+            pltpu.VMEM((n_rows, ffn), bf16),
+            pltpu.VMEM((N_SLOT, ffn, chunk), bf16),
+            dma(()),
+            dma((N_CHUNK,)),
+            dma((N_SLOT,)),
+            dma((5, N_CHUNK)),
+            dma((5, N_CHUNK)),
+            dma((5, N_CHUNK)),
+            dma((5, N_CHUNK)),
+        ],
+        compiler_params=pltpu.CompilerParams(collective_id=0, has_side_effects=True,
+                                             vmem_limit_bytes=67043328),
+        name='layer_tail',
+    )(attn_out, resid_in, gain_mlp.reshape(1, width), w_out, w_gate.T, w_up.T, w_down)
 
 
 def solution(mesh):
@@ -82,13 +390,7 @@
                     w_out, gain_mlp, w_gate, w_up, w_down):
         attn_out, k_full, v_full = attention_block(resid_in, positions, k_cache, v_cache,
                                                    gain_attn, w_query, w_key, w_value)
-        y_part = jnp.dot(attn_out, w_out, preferred_element_type=jnp.float32)
-        y_sum = lax.psum(y_part, 'tp')
-        resid_mid = (resid_in.astype(jnp.float32) + y_sum).astype(jnp.bfloat16)
-        hidden = gated_hidden(rms_norm(resid_mid, gain_mlp), w_gate, w_up)
-        z_part = jnp.dot(hidden, w_down, preferred_element_type=jnp.float32)
-        z_sum = lax.psum(z_part, 'tp')
-        resid_out = (resid_mid.astype(jnp.float32) + z_sum).astype(jnp.bfloat16)
+        resid_out = layer_tail(attn_out, resid_in, gain_mlp, w_out, w_gate, w_up, w_down)
         return resid_out, k_full, v_full
 
     row_spec = P('dp', None)

time: 267 us -> 176 us (0.66)
  waiting for transfers between devices: 141 us -> 0 us
  Pallas kernels: 0 us -> 139 us
  matrix products: 89.6 us -> 18.7 us
  between operations: 14.3 us -> 0.81 us
  other arithmetic: 19.1 us -> 10.4 us
  local copies, waits for them, and re-layouts: 2.73 us -> 6.74 us
    psum x2 -> x0, waiting for transfers between devices: 141 us -> none  [the longest x1 71.6 us: layer_local(): y_sum = lax.psum(y_part, 'tp')]
    pallas_call x0 -> x1, Pallas kernels: none -> 139 us  [layer_tail(): pl.pallas_call(tail_kernel, out_shape=jax.ShapeDtypeStruct((n_rows, width...]
    dot_general x3 -> x0, matrix products: 71.5 us -> none  [the longest x1 41.8 us: layer_local(): z_part = jnp.dot(hidden, w_down, preferred_element_type=jnp.float32)]
    convert_element_type x1 -> x0, other arithmetic: 4.6 us -> none  [layer_local(): resid_out = (resid_mid.astype(jnp.float32) + z_sum).astype(jnp.bfloat16)]
    unnamed x21 -> x17, local copies, waits for them, and re-layouts: 2.62 us -> 5.99 us
    reduce_sum x2 -> x1, other arithmetic: 5.66 us -> 2.52 us  [rms_norm(): mean_sq = jnp.mean(rows_f * rows_f, axis=-1, keepdims=True)]
  transfers between devices with their start and end apart: 2 -> 0, of which waited for: 2 -> 0; matrix products, arithmetic and copies ran while one was open for 0% -> 0% of each run, Pallas kernels for 0% -> 0%
where the time goes in v1:
time: 176 us
  Pallas kernels  139 us (79%)
  matrix products  18.7 us (11%)
  other arithmetic  10.4 us (6%)
  local copies, waits for them, and re-layouts  6.74 us (4%)
    pallas_call x1, Pallas kernels, layer_tail(): pl.pallas_call(tail_kernel, out_shape=jax.ShapeDtypeStruct((n_rows, width...  139 us
    dot_general x1, matrix products, attention_block(): jnp.dot(normed, w_query, preferred_element_type=jnp.float32)  8.29 us
    unnamed x17, local copies, waits for them, and re-layouts  5.99 us
    select_n x1, other arithmetic, attention_block(): k_full = jnp.where(slot_hit, key_new[:, None], k_cache)  5.08 us
    dot_general x1, matrix products, attention_block(): jnp.einsum('bkgs,bskd->bkgd', attn_prob, v_full, preferred_element_type=j...  4 us

profile of v1, /device:TPU:0, one launch (start us, length us, event | category | flops | bytes accessed | tf_op | source)
XLA Modules:
  0.0 175.8 jit_solution(14450017499824316245)
XLA Ops:
  0.6 0.0 copy-start.1
  0.7 0.8 convert_element_type.57
  1.5 2.5 %fusion.1 = f32[128]{0:T(128)S(1)} fusion(bf16[128,8192]{1,0:T(8,128)(2,1)} %resid_hbm.1), kind=kLoop, calls=%fused_computation.3 | loop fusion | flops 3145600 | bytes 2097664 | tf_op jit(solution)/shard_map/reduce_sum | solution.py:19
  4.0 0.7 convert_element_type.52
  4.8 3.0 %convolution_convert_fusion.1 = bf16[128,128]{1,0:T(8,128)(2,1)S(1)} fusion(bf16[8192,128]{1,0:T(8,128)(2,1)} %param.20, bf16[128,8192]{1,0:T(8,128)(2,1)} %resid_hbm.1, f32[8192]{0:T(1024)S(1)} %convert_element_type.52, f32[128]{0:T(128)S(1)} %add_rsqrt_fusion), kind=kOutput, calls=%fused_computation.20 | convolution fusion | flops 272646144 | bytes 4260352 | tf_op jit(solution)/shard_map/dot_general | solution.py:55
  7.8 0.6 reshape.246.gain_ref
  8.4 0.1 iota_compare_fusion.1
  8.5 1.1 fusion.22
  9.7 0.2 fusion.36
  9.9 0.1 copy.16
  10.0 0.3 multiply_cosine_fusion
  10.3 0.0 copy-start.2
  10.3 0.0 copy-start.3
  10.4 8.3 %fusion.20 = f32[16,8,8,128]{3,1,2,0:T(8,128)S(1)} fusion(bf16[8192,1024]{1,0:T(8,128)(2,1)} %param.18, bf16[128,8192]{1,0:T(8,128)(2,1)S(1)} %copy-done.1, f32[8192]{0:T(1024)S(1)} %convert_element_type.52, f32[128]{0:T(128)S(1)} %add_rsqrt_fusion), kind=kOutput, calls=%fused_computation.19 | convolution fusion | flops 2151940096 | bytes 19431936 | tf_op jit(solution)/shard_map/dot_general | solution.py:53
  18.7 0.1 copy.17
  18.8 0.3 subtract_convert_fusion
  19.1 5.1 %broadcast_select_fusion.1 = (bf16[128,128,1,128]{3,1,2,0:T(8,128)(2,1)S(1)}, bf16[128,128,1,128]{3,1,2,0:T(8,128)(2,1)}) fusion(bf16[128,128,1,128]{3,1,2,0:T(8,128)(2,1)S(1)} %copy-done.2, pred[128,128]{1,0:T(8,128)(4,1)S(1)} %get-tuple-element.12, bf16[128,128]{1,0:T(8,128)(2,1)S(1)} %copy.16, bf16[128,128,1,128]{3,1,2,0:T(8,128)(2,1)S(1)} %copy-done.3, ...), kind=kLoop, calls=%fused_computation.11 | loop fusion | flops 4194304 | bytes 16859136 | tf_op jit(solution)/shard_map/jit(_where)/select_n | solution.py:64
  24.2 2.0 %copy-done = bf16[128,128,1,128]{3,1,2,0:T(8,128)(2,1)} copy-done((bf16[128,128,1,128]{3,1,2,0:T(8,128)(2,1)}, bf16[128,128,1,128]{3,1,2,0:T(8,128)(2,1)S(1)}, u32[]{:S(2)}) %copy-start) | copy-done | bytes 4194328
  26.2 2.3 %fusion.13 = f32[128,8,128]{2,1,0:T(8,128)S(1)} fusion(bf16[128,128,1,128]{3,1,2,0:T(8,128)(2,1)S(1)} %get-tuple-element.17, bf16[128,8,64]{2,1,0:T(8,128)(2,1)S(1)} %get-tuple-element.4, bf16[128,8,64]{2,1,0:T(8,128)(2,1)S(1)} %get-tuple-element.3, pred[128,128]{1,0:T(8,128)(4,1)S(1)} %get-tuple-element.11), kind=kOutput, calls=%fused_computation.15 | convolution fusion | flops 34340864 | bytes 4997120 | tf_op jit(solution)/shard_map/bkgd,bskd->bkgs/dot_general | solution.py:66
  28.5 0.4 fusion.41
  28.9 4.0 %fusion.16 = bf16[128,8,128]{2,1,0:T(8,128)(2,1)S(1)} fusion(bf16[128,128,1,128]{3,1,2,0:T(8,128)(2,1)} %get-tuple-element.18, f32[128,8]{1,0:T(8,128)S(1)} %fusion.41, f32[128,8,128]{2,1,0:T(8,128)S(1)} %fusion.13), kind=kOutput, calls=%fused_computation.16 | convolution fusion | flops 34079872 | bytes 4984832 | tf_op jit(solution)/shard_map/bkgs,bskd->bkgd/dot_general | solution.py:71
  32.9 0.8 copy.20
  33.6 139.1 %layer_tail.1 = bf16[128,8192]{1,0:T(8,128)(2,1)} custom-call(bf16[128,1024]{1,0:T(8,128)(2,1)} %bitcast.38, bf16[128,8192]{1,0:T(8,128)(2,1)} %resid_hbm.1, bf16[1,8192]{1,0:T(2,128)(2,1)} %reshape.246.gain_ref, bf16[1024,8192]{1,0:T(8,128)(2,1)} %w_out_hbm.1, bf16[2752,8192]{1,0:T(8,128)(2,1)} %bitcast.35, bf16[2752,8192]{1,0:T(8,128)(2,1)} %bitcast.36, ...), custom_call_target="tpu_custom_call" | custom-call | tf_op jit(solution)/shard_map/layer_tail/pallas_call | solution.py:354
  172.7 3.1 %copy.22 = bf16[128,8192]{1,0:T(8,128)(2,1)} copy(bf16[128,8192]{1,0:T(8,128)(2,1)} %layer_tail.1) | data formatting | bytes 4194304
  (13 shorter events, 0.1 us)
Async XLA Ops:
  0.6 7.9 %copy-start.1 = (bf16[128,8192]{1,0:T(8,128)(2,1)S(1)}, bf16[128,8192]{1,0:T(8,128)(2,1)}, u32[]{:S(2)}) copy-start(bf16[128,8192]{1,0:T(8,128)(2,1)} %resid_hbm.1) | copy-start | bytes 6291460
  0.6 7.8 %copy-start.5 = (s32[128]{0:T(128)S(1)}, s32[128]{0:T(128)}, u32[]{:S(2)}) copy-start(s32[128]{0:T(128)} %param.14) | copy-start | bytes 1540
  0.7 7.1 %copy-start.4 = (bf16[8192]{0:T(1024)(128)(2,1)S(1)}, bf16[8192]{0:T(1024)(128)(2,1)}, u32[]{:S(2)}) copy-start(bf16[8192]{0:T(1024)(128)(2,1)} %param.22) | copy-start | bytes 49156
  0.7 7.9 %copy-start.6 = (bf16[8192,128]{1,0:T(8,128)(2,1)S(1)}, bf16[8192,128]{1,0:T(8,128)(2,1)}, u32[]{:S(2)}) copy-start(bf16[8192,128]{1,0:T(8,128)(2,1)} %param.19) | copy-start | bytes 6291460
  10.3 8.7 %copy-start.2 = (bf16[128,128,1,128]{3,1,2,0:T(8,128)(2,1)S(1)}, bf16[128,128,1,128]{3,1,2,0:T(8,128)(2,1)}, u32[]{:S(2)}) copy-start(bf16[128,128,1,128]{3,1,2,0:T(8,128)(2,1)} %param.15) | copy-start | bytes 12582916
  10.3 8.7 %copy-start.3 = (bf16[128,128,1,128]{3,1,2,0:T(8,128)(2,1)S(1)}, bf16[128,128,1,128]{3,1,2,0:T(8,128)(2,1)}, u32[]{:S(2)}) copy-start(bf16[128,128,1,128]{3,1,2,0:T(8,128)(2,1)} %param.16) | copy-start | bytes 12582916
  24.2 2.0 %copy-start = (bf16[128,128,1,128]{3,1,2,0:T(8,128)(2,1)}, bf16[128,128,1,128]{3,1,2,0:T(8,128)(2,1)S(1)}, u32[]{:S(2)}) copy-start(bf16[128,128,1,128]{3,1,2,0:T(8,128)(2,1)S(1)} %get-tuple-element.17) | copy-start | bytes 12582916

commit v2 on v1

--- a/solution.py
+++ b/solution.py
@@ -14,63 +14,184 @@
 ORIG_CTX = 8192.0
 
 
-def rms_norm(rows_in, gain):
-    rows_f = rows_in.astype(jnp.float32)
-    mean_sq = jnp.mean(rows_f * rows_f, axis=-1, keepdims=True)
-    return (rows_f * lax.rsqrt(mean_sq + EPS) * gain.astype(jnp.float32)).astype(jnp.bfloat16)
-
-
-def rope_tables(positions, head_dim):
+def rope_freqs(head_dim):
     half_dim = head_dim // 2
-    exponents = jnp.arange(half_dim, dtype=jnp.float32) * (2.0 / head_dim)
+    exponents = (jnp.arange(head_dim, dtype=jnp.int32) % half_dim).astype(jnp.float32) * (2.0 / head_dim)
     inv_freq = 1.0 / jnp.power(ROPE_THETA, exponents)
     wavelen = (2.0 * math.pi) / inv_freq
     smooth = (ORIG_CTX / wavelen - LOW_FACTOR) / (HIGH_FACTOR - LOW_FACTOR)
     blended = (1.0 - smooth) * inv_freq / ROPE_FACTOR + smooth * inv_freq
     inv_freq = jnp.where(wavelen < ORIG_CTX / HIGH_FACTOR, inv_freq,
                          jnp.where(wavelen > ORIG_CTX / LOW_FACTOR, inv_freq / ROPE_FACTOR, blended))
-    angles = positions.astype(jnp.float32)[:, None] * inv_freq[None, :]
-    return jnp.cos(angles), jnp.sin(angles)
-
-
-def apply_rope(vectors, cos_t, sin_t):
-    half_dim = vectors.shape[-1] // 2
-    lower_half = vectors[..., :half_dim]
-    upper_half = vectors[..., half_dim:]
-    cos_b = cos_t[:, None, :]
-    sin_b = sin_t[:, None, :]
-    return jnp.concatenate([lower_half * cos_b - upper_half * sin_b,
-                            upper_half * cos_b + lower_half * sin_b], axis=-1)
-
-
-def attention_block(resid_in, positions, k_cache, v_cache, gain_attn, w_query, w_key, w_value):
-    n_seqs = resid_in.shape[0]
-    cache_len = k_cache.shape[1]
-    kv_heads = k_cache.shape[2]
-    head_dim = k_cache.shape[3]
-    group_size = w_query.shape[1] // (kv_heads * head_dim)
-    normed = rms_norm(resid_in, gain_attn)
-    queries = jnp.dot(normed, w_query, preferred_element_type=jnp.float32).astype(jnp.bfloat16)
-    key_new = jnp.dot(normed, w_key, preferred_element_type=jnp.float32).astype(jnp.bfloat16)
-    value_new = jnp.dot(normed, w_value, preferred_element_type=jnp.float32).astype(jnp.bfloat16)
-    cos_t, sin_t = rope_tables(positions, head_dim)
-    queries = apply_rope(queries.reshape(n_seqs, kv_heads * group_size, head_dim).astype(jnp.float32), cos_t, sin_t)
-    queries = queries.astype(jnp.bfloat16).reshape(n_seqs, kv_heads, group_size, head_dim)
-    key_new = apply_rope(key_new.reshape(n_seqs, kv_heads, head_dim).astype(jnp.float32), cos_t, sin_t)
-    key_new = key_new.astype(jnp.bfloat16)
-    value_new = value_new.reshape(n_seqs, kv_heads, head_dim)
-    slot_iota = lax.broadcasted_iota(jnp.int32, (n_seqs, cache_len), 1)
-    slot_hit = (slot_iota == positions[:, None])[:, :, None, None]
-    k_full = jnp.where(slot_hit, key_new[:, None], k_cache)
-    v_full = jnp.where(slot_hit, value_new[:, None], v_cache)
-    scores = jnp.einsum('bkgd,bskd->bkgs', queries, k_full, preferred_element_type=jnp.float32)
-    scores = scores * (1.0 / math.sqrt(head_dim))
-    valid = (slot_iota <= positions[:, None])[:, None, None, :]
-    scores = jnp.where(valid, scores, -jnp.inf)
-    attn_prob = jax.nn.softmax(scores, axis=-1).astype(jnp.bfloat16)
-    attn_out = jnp.einsum('bkgs,bskd->bkgd', attn_prob, v_full, preferred_element_type=jnp.float32)
-    attn_out = attn_out.astype(jnp.bfloat16).reshape(n_seqs, kv_heads * group_size * head_dim)
-    return attn_out, k_full, v_full
+    return inv_freq[None, :]
+
+
+def front_kernel(pos_ref, resid_ref, gain_ref, pos_row_ref, freq_ref, w_query_hbm, w_key_hbm, w_value_hbm,
+                 k_in_hbm, v_in_hbm, attn_ref, k_out_hbm, v_out_hbm,
+                 w_buf, acc, k_buf, v_buf, q_rows, o_rows, k_new, v_new, gain_f, cos_ref, sin_ref,
+                 w_sem, cache_sem, out_sem):
+    n_seqs, width = resid_ref.shape
+    depth, q_width = w_buf.shape[1], w_query_hbm.shape[1]
+    head_dim = k_new.shape[1]
+    group_size = q_width // head_dim
+    n_block = n_seqs // SEQ_BLOCK
+
+    def w_copies(c):
+        span = pl.ds(pl.multiple_of(c * depth, depth), depth)
+        copies = []
+        for i, (src, lo, size) in enumerate(((w_query_hbm, 0, q_width), (w_key_hbm, q_width, head_dim),
+                                             (w_value_hbm, q_width + head_dim, head_dim))):
+            copies.append(pltpu.make_async_copy(src.at[span], w_buf.at[c, :, pl.ds(lo, size)], w_sem.at[i, c]))
+        return copies
+
+    def block(b):
+        return pl.ds(pl.multiple_of(b * SEQ_BLOCK, SEQ_BLOCK), SEQ_BLOCK)
+
+    def in_copies(b):
+        return (pltpu.make_async_copy(k_in_hbm.at[block(b)], k_buf.at[block(b)], cache_sem.at[0, b]),
+                pltpu.make_async_copy(v_in_hbm.at[block(b)], v_buf.at[block(b)], cache_sem.at[1, b]))
+
+    def out_copies(b):
+        return (pltpu.make_async_copy(k_buf.at[block(b)], k_out_hbm.at[block(b)], out_sem.at[0, b]),
+                pltpu.make_async_copy(v_buf.at[block(b)], v_out_hbm.at[block(b)], out_sem.at[1, b]))
+
+    n_w = width // depth
+    for c in range(n_w):
+        for copy in w_copies(c):
+            copy.start()
+    gain_f[...] = gain_ref[...].astype(jnp.float32)
+
+    def cols(c):
+        return pl.ds(pl.multiple_of(c * depth, depth), depth)
+
+    def add_squares(c, total):
+        part = resid_ref[:, cols(c)].astype(jnp.float32)
+        part = part * part
+        for j in range(depth // 128):
+            total = total + part[:, j * 128:(j + 1) * 128]
+        return total
+
+    squares = lax.fori_loop(0, n_w, add_squares, jnp.zeros((n_seqs, 128), jnp.float32))
+    scale = lax.rsqrt(jnp.sum(squares, axis=-1, keepdims=True) * (1.0 / width) + EPS)
+    acc[...] = jnp.zeros_like(acc)
+    angles = (jnp.broadcast_to(pos_row_ref[...].astype(jnp.float32), (n_seqs, n_seqs)).T[:, :1]
+              * freq_ref[...])
+    cos_f = jnp.cos(angles)
+    sin_f = jnp.sin(angles)
+    sin_f = jnp.where(lax.broadcasted_iota(jnp.int32, sin_f.shape, 1) < head_dim // 2, -sin_f, sin_f)
+    cos_ref[...] = cos_f
+    sin_ref[...] = sin_f
+    per_step = n_block // (n_w // 2)
+
+    def project(c, carry):
+        rows_f = resid_ref[:, cols(c)].astype(jnp.float32) * scale
+        normed = jnp.concatenate(
+            [rows_f[:, j * 128:(j + 1) * 128] * gain_f[pl.ds(c * (depth // 128) + j, 1), :]
+             for j in range(depth // 128)], axis=-1).astype(jnp.bfloat16)
+        for copy in w_copies(c):
+            copy.wait()
+
+        @pl.when(c >= n_w // 2)
+        def _():
+            for i in range(per_step):
+                for copy in in_copies((c - n_w // 2) * per_step + i):
+                    copy.start()
+
+        acc[...] += jnp.dot(normed, w_buf[c], preferred_element_type=jnp.float32)
+        return carry
+
+    lax.fori_loop(0, n_w, project, 0)
+
+    def rotate(cols_f):
+        values = cols_f.astype(jnp.bfloat16).astype(jnp.float32)
+        turned = values * cos_ref[...] + pltpu.roll(values, head_dim // 2, 1) * sin_ref[...]
+        return turned.astype(jnp.bfloat16).astype(jnp.float32)
+
+    for j in range(group_size):
+        q_rows[pl.ds(j, n_seqs, stride=group_size), :] = rotate(acc[:, j * head_dim:(j + 1) * head_dim])
+    k_new[...] = rotate(acc[:, q_width:q_width + head_dim])
+    v_new[...] = acc[:, q_width + head_dim:].astype(jnp.bfloat16).astype(jnp.float32)
+    inv_sqrt = 1.0 / math.sqrt(head_dim)
+
+    def attend(b, carry):
+        for copy in in_copies(b):
+            copy.wait()
+        for i in range(SEQ_BLOCK):
+            seq = b * SEQ_BLOCK + i
+            pos = pos_ref[seq]
+            base = pl.multiple_of(pos // 16 * 16, 16)
+            hit = lax.broadcasted_iota(jnp.int32, (16, head_dim), 0) == pos - base
+            for buf, new in ((k_buf, k_new), (v_buf, v_new)):
+                old = buf[seq, pl.ds(base, 16), :].astype(jnp.float32)
+                buf[seq, pl.ds(base, 16), :] = jnp.where(hit, new[pl.ds(seq, 1), :], old).astype(jnp.bfloat16)
+        for copy in out_copies(b):
+            copy.start()
+        rows, probs = [], []
+        for i in range(SEQ_BLOCK):
+            seq = b * SEQ_BLOCK + i
+            rows.append(pl.ds(pl.multiple_of(seq * group_size, group_size), group_size))
+            query = q_rows[rows[i], :].astype(jnp.bfloat16)
+            scores = lax.dot_general(query, k_buf[seq], (((1,), (1,)), ((), ())),
+                                     preferred_element_type=jnp.float32) * inv_sqrt
+            valid = lax.broadcasted_iota(jnp.int32, scores.shape, 1) <= pos_ref[seq]
+            scores = jnp.where(valid, scores, -jnp.inf)
+            exps = jnp.exp(scores - jnp.max(scores, axis=-1, keepdims=True))
+            probs.append((exps / jnp.sum(exps, axis=-1, keepdims=True)).astype(jnp.bfloat16))
+        for i in range(SEQ_BLOCK):
+            o_rows[rows[i], :] = jnp.dot(probs[i], v_buf[b * SEQ_BLOCK + i], preferred_element_type=jnp.float32)
+        return carry
+
+    lax.fori_loop(0, n_block, attend, 0)
+    for j in range(group_size):
+        attn_ref[:, j * head_dim:(j + 1) * head_dim] = (
+            o_rows[pl.ds(j, n_seqs, stride=group_size), :].astype(jnp.bfloat16))
+    for b in range(n_block):
+        for copy in out_copies(b):
+            copy.wait()
+
+
+SEQ_BLOCK = 16
+FRONT_DEPTH = 1024
+
+
+def layer_front(resid_in, positions, k_cache, v_cache, gain_attn, w_query, w_key, w_value):
+    n_seqs, width = resid_in.shape
+    cache_len, head_dim = k_cache.shape[1], k_cache.shape[3]
+    q_width = w_query.shape[1]
+    f32, bf16 = jnp.float32, jnp.bfloat16
+    vmem = pl.BlockSpec(memory_space=pltpu.VMEM)
+    hbm = pl.BlockSpec(memory_space=pl.ANY)
+    dma = pltpu.SemaphoreType.DMA
+    n_w, n_block = width // FRONT_DEPTH, n_seqs // SEQ_BLOCK
+    flat = (n_seqs, cache_len, head_dim)
+    attn_out, k_out, v_out = pl.pallas_call(
+        front_kernel,
+        out_shape=(jax.ShapeDtypeStruct((n_seqs, q_width), bf16),
+                   jax.ShapeDtypeStruct(flat, bf16), jax.ShapeDtypeStruct(flat, bf16)),
+        in_specs=[pl.BlockSpec(memory_space=pltpu.SMEM), vmem, vmem, vmem, vmem, hbm, hbm, hbm, hbm, hbm],
+        out_specs=(vmem, hbm, hbm),
+        scratch_shapes=[
+            pltpu.VMEM((n_w, FRONT_DEPTH, q_width + 2 * head_dim), bf16),
+            pltpu.VMEM((n_seqs, q_width + 2 * head_dim), f32),
+            pltpu.VMEM(flat, bf16),
+            pltpu.VMEM(flat, bf16),
+            pltpu.VMEM((n_seqs * q_width // head_dim, head_dim), f32),
+            pltpu.VMEM((n_seqs * q_width // head_dim, head_dim), f32),
+            pltpu.VMEM((n_seqs, head_dim), f32),
+            pltpu.VMEM((n_seqs, head_dim), f32),
+            pltpu.VMEM((width // 128, 128), f32),
+            pltpu.VMEM((n_seqs, head_dim), f32),
+            pltpu.VMEM((n_seqs, head_dim), f32),
+            dma((3, n_w)),
+            dma((2, n_block)),
+            dma((2, n_block)),
+        ],
+        compiler_params=pltpu.CompilerParams(vmem_limit_bytes=67043328),
+        name='layer_front',
+    )(positions, resid_in, gain_attn.reshape(width // 128, 128), positions[None, :],
+      rope_freqs(head_dim), w_query, w_key, w_value,
+      k_cache.reshape(flat), v_cache.reshape(flat))
+    return attn_out, k_out.reshape(k_cache.shape), v_out.reshape(v_cache.shape)
 
 
 N_CHUNK = 16
@@ -79,7 +200,7 @@
 
 
 def tail_kernel(attn_ref, resid_hbm, gain_ref, w_out_hbm, gate_t_hbm, up_t_hbm, w_down_hbm, out_ref,
-                part, from_core, from_x1, from_y1, from_x2, from_y2, gathered, mid, sq_sum, resid_own,
+                part, from_core, from_x1, from_y1, from_x2, from_y2, gathered, mid, sq_sum, resid_own, gain_f,
                 gate_acc, up_acc, hidden, ring,
                 resid_sem, out_sem, ring_sem, rs_send, rs_recv, ag_send, ag_recv):
     n_chunk, chunk = N_CHUNK, part.shape[-1]
@@ -140,13 +261,9 @@
 
     row0 = pl.multiple_of(64 * k + 32 * x + 16 * y, 16)
     resid_copy = pltpu.make_async_copy(resid_hbm.at[pl.ds(row0, rows)], resid_own, resid_sem)
-    for c in range(2):
+    resid_copy.start()
+    for c in range(OUT_AHEAD):
         out_copy(c).start()
-    resid_copy.start()
-    for c in range(2, n_chunk):
-        out_copy(c).start()
-    for j in range(first_mlp, N_SLOT):
-        (up_copy if (j - first_mlp) % 2 else gate_copy)((j - first_mlp) // 2).start()
 
     barrier = pltpu.get_barrier_semaphore()
     for nbr in (core_nbr, x_nbr, y_nbr):
@@ -243,9 +360,12 @@
             copy(c).wait_send()
         return block
 
+    gain_f[...] = gain_ref[...].astype(jnp.float32)
+    sq_sum[...] = jnp.zeros_like(sq_sum)
+    gate_acc[...] = jnp.zeros_like(gate_acc)
+    up_acc[...] = jnp.zeros_like(up_acc)
+    resid_copy.wait()
     pl.semaphore_wait(barrier, 3)
-    sq_sum[...] = jnp.zeros_like(sq_sum)
-    resid_copy.wait()
 
     def proj(c):
         out_copy(c).wait()
@@ -254,6 +374,14 @@
         part[c] = res.reshape(part.shape[1:])
         rs_core(c).start()
 
+        @pl.when(c + OUT_AHEAD < n_chunk)
+        def _():
+            out_copy(c + OUT_AHEAD).start()
+
+        @pl.when(first_mlp + c < N_SLOT)
+        def _():
+            start_load(first_mlp + c)
+
         @pl.when(c % 2 == 1)
         def _():
             start_load(c // 2 + N_SLOT)
@@ -265,21 +393,20 @@
         sq_sum[...] += x1 * x1
 
     def rs_body(s, carry):
-        stage(s, RS_LAG[0], rs_stage1)
-        stage(s, RS_LAG[1], rs_stage2)
-        stage(s, RS_LAG[2], finish_mid)
+        stage(s, RS1_LAG[2], finish_mid)
+        stage(s, RS1_LAG[1], rs_stage2)
+        stage(s, RS1_LAG[0], rs_stage1)
         stage(s, 0, proj)
         return carry
 
-    lax.fori_loop(0, n_chunk + RS_LAG[2], rs_body, 0)
+    lax.fori_loop(0, n_chunk + RS1_LAG[2], rs_body, 0)
 
     mean_sq = jnp.sum(sq_sum[...], axis=-1, keepdims=True) * (1.0 / (n_chunk * chunk))
     scale = lax.rsqrt(mean_sq + EPS)
-    gate_acc[...] = jnp.zeros_like(gate_acc)
-    up_acc[...] = jnp.zeros_like(up_acc)
 
     def send_normed(c):
-        normed = (mid[c] * scale * gain_ref[:, cols(c)].astype(jnp.float32)).astype(jnp.bfloat16)
+        gain = jnp.concatenate([gain_f[pl.ds(c * (chunk // 128) + j, 1), :] for j in range(chunk // 128)], axis=-1)
+        normed = (mid[c] * scale * gain).astype(jnp.bfloat16)
         gathered[c, k, x, y] = normed.astype(jnp.float32)
         ag_x(c).start()
         ag_y(c).start()
@@ -288,22 +415,24 @@
         block = ag_stage3(c).astype(jnp.bfloat16)
         for copy, acc, j in ((gate_copy, gate_acc, first_mlp + 2 * c), (up_copy, up_acc, first_mlp + 2 * c + 1)):
             copy(c).wait()
-            acc[...] += lax.dot_general(block, ring[j % N_SLOT], (((1,), (1,)), ((), ())),
+            acc[...] += lax.dot_general(ring[j % N_SLOT], block, (((1,), (1,)), ((), ())),
                                         preferred_element_type=jnp.float32)
             start_load(j + N_SLOT)
 
     def ag_body(s, carry):
-        stage(s, AG_LAG[0], ag_stage1)
-        stage(s, AG_LAG[1], ag_stage2)
         stage(s, 0, send_normed)
-        stage(s, AG_LAG[2], gate_up)
+        stage(s, AG1_LAG[0], ag_stage1)
+        stage(s, AG1_LAG[1], ag_stage2)
+        stage(s, AG1_LAG[2], gate_up)
         return carry
 
-    lax.fori_loop(0, n_chunk + AG_LAG[2], ag_body, 0)
-
-    gate = gate_acc[...].astype(jnp.bfloat16).astype(jnp.float32)
-    up = up_acc[...].astype(jnp.bfloat16).astype(jnp.float32)
-    hidden[...] = (jax.nn.silu(gate) * up).astype(jnp.bfloat16)
+    lax.fori_loop(0, n_chunk + AG1_LAG[2], ag_body, 0)
+
+    for lo in range(0, hidden.shape[1], 128):
+        span = slice(lo, min(lo + 128, hidden.shape[1]))
+        gate = gate_acc[span, :].astype(jnp.bfloat16).astype(jnp.float32)
+        up = up_acc[span, :].astype(jnp.bfloat16).astype(jnp.float32)
+        hidden[:, span] = (jax.nn.silu(gate) * up).T.astype(jnp.bfloat16)
 
     def down(c):
         down_copy(c).wait()
@@ -322,23 +451,26 @@
     def store_out(c):
         out_ref[:, cols(c)] = ag_stage3(c).astype(jnp.bfloat16)
 
-    base = RS_LAG[2]
+    base = RS2_LAG[2]
 
     def down_body(s, carry):
-        stage(s, RS_LAG[0], rs_stage1)
-        stage(s, RS_LAG[1], rs_stage2)
+        stage(s, base + AG2_LAG[1], ag_stage2)
+        stage(s, base + AG2_LAG[0], ag_stage1)
         stage(s, base, finish_out)
-        stage(s, base + AG_LAG[0], ag_stage1)
-        stage(s, base + AG_LAG[1], ag_stage2)
+        stage(s, RS2_LAG[1], rs_stage2)
+        stage(s, RS2_LAG[0], rs_stage1)
         stage(s, 0, down)
-        stage(s, base + AG_LAG[2], store_out)
+        stage(s, base + AG2_LAG[2], store_out)
         return carry
 
-    lax.fori_loop(0, n_chunk + base + AG_LAG[2], down_body, 0)
-
-
-RS_LAG = (1, 4, 7)
-AG_LAG = (3, 6, 8)
+    lax.fori_loop(0, n_chunk + base + AG2_LAG[2], down_body, 0)
+
+
+RS1_LAG = (2, 5, 7)
+AG1_LAG = (2, 4, 5)
+RS2_LAG = (2, 4, 6)
+AG2_LAG = (2, 4, 5)
+OUT_AHEAD = 5
 
 
 def layer_tail(attn_out, resid_in, gain_mlp, w_out, w_gate, w_up, w_down):
@@ -367,8 +499,9 @@
             pltpu.VMEM((N_CHUNK, rows, chunk), f32),
             pltpu.VMEM((rows, chunk), f32),
             pltpu.VMEM((rows, width), bf16),
-            pltpu.VMEM((n_rows, ffn), f32),
-            pltpu.VMEM((n_rows, ffn), f32),
+            pltpu.VMEM((width // 128, 128), f32),
+            pltpu.VMEM((ffn, n_rows), f32),
+            pltpu.VMEM((ffn, n_rows), f32),
             pltpu.VMEM((n_rows, ffn), bf16),
             pltpu.VMEM((N_SLOT, ffn, chunk), bf16),
             dma(()),
@@ -382,14 +515,14 @@
         compiler_params=pltpu.CompilerParams(collective_id=0, has_side_effects=True,
                                              vmem_limit_bytes=67043328),
         name='layer_tail',
-    )(attn_out, resid_in, gain_mlp.reshape(1, width), w_out, w_gate.T, w_up.T, w_down)
+    )(attn_out, resid_in, gain_mlp.reshape(width // 128, 128), w_out, w_gate.T, w_up.T, w_down)
 
 
 def solution(mesh):
     def layer_local(resid_in, positions, k_cache, v_cache, gain_attn, w_query, w_key, w_value,
                     w_out, gain_mlp, w_gate, w_up, w_down):
-        attn_out, k_full, v_full = attention_block(resid_in, positions, k_cache, v_cache,
-                                                   gain_attn, w_query, w_key, w_value)
+        attn_out, k_full, v_full = layer_front(resid_in, positions, k_cache, v_cache,
+                                               gain_attn, w_query, w_key, w_value)
         resid_out = layer_tail(attn_out, resid_in, gain_mlp, w_out, w_gate, w_up, w_down)
         return resid_out, k_full, v_full
 

time: 176 us -> 142 us (0.81)
  matrix products: 18.7 us -> 0 us
  other arithmetic: 10.4 us -> 0.53 us
  local copies, waits for them, and re-layouts: 6.74 us -> 3.1 us
  Pallas kernels: 139 us -> 137 us
    pallas_call x1, Pallas kernels: 139 us -> 120 us  [layer_tail(): pl.pallas_call(tail_kernel, out_shape=jax.ShapeDtypeStruct((n_rows, width...]
    dot_general x5 -> x0, matrix products: 18.7 us -> none  [the longest x1 8.29 us: attention_block(): jnp.dot(normed, w_query, preferred_element_type=jnp.float32)]
    pallas_call x0 -> x1, Pallas kernels: none -> 17.2 us  [layer_front(): pl.pallas_call(front_kernel, out_shape=(jax.ShapeDtypeStruct((n_seqs, q_w...]
    select_n x2 -> x1, other arithmetic: 5.1 us -> 0.53 us  [rope_freqs(): jnp.where(wavelen < ORIG_CTX / HIGH_FACTOR, inv_freq, jnp.where(wavelen >...]
    unnamed x17 -> x1, local copies, waits for them, and re-layouts: 5.99 us -> 3.1 us
    reduce_sum x1 -> x0, other arithmetic: 2.52 us -> none  [rms_norm(): mean_sq = jnp.mean(rows_f * rows_f, axis=-1, keepdims=True)]
where the time goes in v2:
time: 142 us
  Pallas kernels  137 us (96%)
  local copies, waits for them, and re-layouts  3.1 us (2%)
    pallas_call x1, Pallas kernels, layer_tail(): pl.pallas_call(tail_kernel, out_shape=jax.ShapeDtypeStruct((n_rows, width...  120 us
    pallas_call x1, Pallas kernels, layer_front(): pl.pallas_call(front_kernel, out_shape=(jax.ShapeDtypeStruct((n_seqs, q_w...  17.2 us
    unnamed x1, local copies, waits for them, and re-layouts  3.1 us

profile of v2, /device:TPU:0, one launch (start us, length us, event | category | flops | bytes accessed | tf_op | source)
XLA Modules:
  0.0 141.6 jit_solution(17805170372248028588)
XLA Ops:
  0.6 0.5 compare_select_fusion.1.freq_ref
  1.2 17.2 %layer_front.1 = (bf16[128,1024]{1,0:T(8,128)(2,1)}, bf16[128,128,128]{2,1,0:T(8,128)(2,1)}, bf16[128,128,128]{2,1,0:T(8,128)(2,1)}) custom-call(s32[128]{0:T(128)} %pos_ref.1, bf16[128,8192]{1,0:T(8,128)(2,1)} %resid_hbm.1, bf16[64,128]{1,0:T(8,128)(2,1)} %bitcast.17, s32[1,128]{1,0:T(1,128)} %bitcast.19, f32[1,128]{1,0:T(1,128)} %compare_select_fusion.1.freq_ref, ...), custom_call_target="tpu_custom_call" | custom-call | tf_op jit(solution)/shard_map/layer_front/pallas_call | solution.py:167
  18.4 120.2 %layer_tail.1 = bf16[128,8192]{1,0:T(8,128)(2,1)} custom-call(bf16[128,1024]{1,0:T(8,128)(2,1)} %get-tuple-element.6.attn_ref, bf16[128,8192]{1,0:T(8,128)(2,1)} %resid_hbm.1, bf16[64,128]{1,0:T(8,128)(2,1)} %bitcast.18, bf16[1024,8192]{1,0:T(8,128)(2,1)} %w_out_hbm.1, bf16[2752,8192]{1,0:T(8,128)(2,1)} %bitcast.13, bf16[2752,8192]{1,0:T(8,128)(2,1)} %bitcast.14, ...), custom_call_target="tpu_custom_call" | custom-call | tf_op jit(solution)/shard_map/layer_tail/pallas_call | solution.py:486
  138.5 3.1 %copy.19 = bf16[128,8192]{1,0:T(8,128)(2,1)} copy(bf16[128,8192]{1,0:T(8,128)(2,1)} %layer_tail.1) | data formatting | bytes 4194304
